TPU v7x, 32 devices: a whole 2x2x4 slice. The times are simulated.
32 devices in a mesh: row: 2 (over x), col: 4 (over z), depth: 4 (over y, core).
Axes of the slice: x: 2, y: 2, z: 4, core: 2. Of those that a mesh axis runs over, the one named last changes fastest.
Arguments:
- acts: bfloat16 [8192, 5120], P(('depth', 'col'), 'row'), may hold values from -6 to 6
- grad_out: bfloat16 [8192, 13824], P(('depth', 'row'), 'col'), may hold values from -6 to 6
- weight: bfloat16 [5120, 13824], P('row', 'col'), may hold values from -0.078125 to 0.078125
- master: float32 [5120, 13824], P(('row', 'depth'), 'col'), may hold values from -0.078125 to 0.078125
- moment_one: float32 [5120, 13824], P(('row', 'depth'), 'col'), may hold values from -4 to 4
- moment_two: float32 [5120, 13824], P(('row', 'depth'), 'col'), may hold values from 0.05 to 2
Outputs:
- grad_in: bfloat16 [8192, 5120], P(('depth', 'col'), 'row')
- new_weight: bfloat16 [5120, 13824], P('row', 'col')
- new_master: float32 [5120, 13824], P(('row', 'depth'), 'col')
- new_moment_one: float32 [5120, 13824], P(('row', 'depth'), 'col')
- new_moment_two: float32 [5120, 13824], P(('row', 'depth'), 'col')
All inputs are finite; a program needn't handle non-finite values.
Results may differ from a plain program's by a relative error of at most 0.0035.
Values may be sent and summed in bfloat16 or wider, within the bound.
A program may use at most 192 MiB of HBM per device.

v0:
```python
import math
import jax
import jax.numpy as jnp
from jax import lax
from jax.sharding import PartitionSpec as P

STEP = 10


def per_device(acts, grad_out, weight, master, moment_one, moment_two):
    whole_acts = lax.all_gather(acts, "col", axis=0, tiled=True)
    tokens_total = acts.shape[0] * lax.axis_size("col") * lax.axis_size("depth")
    whole_cotangent = lax.all_gather(grad_out, "row", axis=0, tiled=True)
    picked = whole_cotangent
    input_sum = lax.psum_scatter(
        lax.dot_general(
            picked, weight, (((1,), (1,)), ((), ())), preferred_element_type=jnp.float32
        ),
        "col",
        scatter_dimension=0,
        tiled=True,
    )
    picked = whole_acts
    grad_sum = lax.psum_scatter(
        lax.dot_general(
            picked, whole_cotangent, (((0,), (0,)), ((), ())), preferred_element_type=jnp.float32
        ).astype(jnp.bfloat16),
        "depth",
        scatter_dimension=0,
        tiled=True,
    ).astype(jnp.float32)
    grad_in = input_sum.astype(jnp.bfloat16)
    grad = grad_sum * jnp.float32(1.0 / math.sqrt(tokens_total))
    new_moment_one = 0.9 * moment_one + 0.1 * grad
    new_moment_two = 0.95 * moment_two + 0.05 * grad * grad
    first_fix = 1.0 - 0.9**STEP
    second_fix = 1.0 - 0.95**STEP
    update = new_moment_one / first_fix / (jnp.sqrt(new_moment_two / second_fix) + 1e-08)
    new_master = master - 0.01 * (update + 0.1 * master)
    new_weight = lax.all_gather(new_master.astype(jnp.bfloat16), "depth", axis=0, tiled=True)
    return (grad_in, new_weight, new_master, new_moment_one, new_moment_two)


def solution(mesh):
    placed = (
        P(("depth", "col"), "row"),
        P(("depth", "row"), "col"),
        P("row", "col"),
        P(("row", "depth"), "col"),
        P(("row", "depth"), "col"),
        P(("row", "depth"), "col"),
    )
    return jax.shard_map(
        per_device,
        mesh=mesh,
        in_specs=placed,
        out_specs=(
            P(("depth", "col"), "row"),
            P("row", "col"),
            P(("row", "depth"), "col"),
            P(("row", "depth"), "col"),
            P(("row", "depth"), "col"),
        ),
        check_vma=False,
    )
```

profile of v0, /device:TPU:0, one launch (start us, length us, event | category | flops | bytes accessed | tf_op | source)
XLA Modules:
  0.0 1031.1 jit_solution(5081694535935332860)
XLA Ops:
  7.2 0.0 all-gather.4.cloned.1.call-start
  7.2 0.7 all-gather.4.cloned.1.call-update
  7.9 0.0 all-gather.6.cloned.1.call-start
  7.9 0.7 all-gather.6.cloned.1.call-update
  8.6 0.0 reduce-scatter.5.cloned.1.call-start
  8.7 173.3 %all-gather.4.cloned.1.call-done = bf16[2048,3456]{1,0:T(8,128)(2,1)} async-done(((bf16[1024,3456]{1,0:T(8,128)(2,1)}), bf16[2048,3456]{1,0:T(8,128)(2,1)}) %all-gather.4.cloned.1.call-update) | async-done | bytes 14155792 | tf_op jit(solution)/shard_map/all_gather | solution.py:13
  182.0 185.5 %all-gather.6.cloned.1.call-done = bf16[2048,2560]{1,0:T(8,128)(2,1)} async-done(((bf16[512,2560]{1,0:T(8,128)(2,1)}), bf16[2048,2560]{1,0:T(8,128)(2,1)}) %all-gather.6.cloned.1.call-update) | async-done | bytes 10485776 | tf_op jit(solution)/shard_map/all_gather | solution.py:11
  367.5 45.6 %convolution_convert_fusion = bf16[2560,3456]{1,0:T(8,128)(2,1)} fusion(bf16[2048,2560]{1,0:T(8,128)(2,1)} %all-gather.6.cloned.1.call-done, bf16[2048,3456]{1,0:T(8,128)(2,1)} %all-gather.4.cloned.1.call-done), kind=kOutput, calls=%fused_computation | convolution fusion | flops 36247633920 | bytes 42336256 | tf_op jit(solution)/shard_map/dot_general | solution.py:25
  413.1 0.0 reduce-scatter.5.cloned.1.call-update
  413.2 0.0 reduce-scatter.3.cloned.1.call-start
  413.2 47.3 %fusion.6 = f32[2048,2560]{1,0:T(8,128)} fusion(bf16[2048,3456]{1,0:T(8,128)(2,1)} %all-gather.4.cloned.1.call-done, bf16[2560,3456]{1,0:T(8,128)(2,1)} %param.8), kind=kOutput, calls=%fused_computation.9 | convolution fusion | flops 36238786560 | bytes 52822016 | tf_op jit(solution)/shard_map/dot_general | solution.py:16
  460.5 0.0 reduce-scatter.3.cloned.1.call-update
  460.5 0.2 all-gather.8.cloned.1.call-start
  460.8 81.3 %reduce-scatter.5.cloned.1.call-done = bf16[640,3456]{1,0:T(8,128)(2,1)} async-done(((bf16[2560,3456]{1,0:T(8,128)(2,1)}), bf16[640,3456]{1,0:T(8,128)(2,1)}) %reduce-scatter.5.cloned.1.call-update) | async-done | bytes 4423696 | tf_op jit(solution)/shard_map/reduce_scatter | solution.py:24
  542.1 23.0 %fusion.3 = (bf16[640,3456]{1,0:T(8,128)(2,1)}, f32[640,3456]{1,0:T(8,128)}, f32[640,3456]{1,0:T(8,128)}, f32[640,3456]{1,0:T(8,128)}) fusion(f32[640,3456]{1,0:T(8,128)} %param.9, bf16[640,3456]{1,0:T(8,128)(2,1)} %reduce-scatter.5.cloned.1.call-done, f32[640,3456]{1,0:T(8,128)} %param.10, f32[640,3456]{1,0:T(8,128)} %param.11), kind=kLoop, calls=%fused_computation.8 | loop fusion | flops 39813120 | bytes 61931520 | tf_op jit(solution)/shard_map/convert_element_type | solution.py:40
  565.1 0.0 all-gather.8.cloned.1.call-update
  565.2 326.6 %reduce-scatter.3.cloned.1.call-done = f32[512,2560]{1,0:T(8,128)} async-done(((f32[2048,2560]{1,0:T(8,128)}), f32[512,2560]{1,0:T(8,128)}) %reduce-scatter.3.cloned.1.call-update) | async-done | bytes 5242896 | tf_op jit(solution)/shard_map/reduce_scatter | solution.py:15
  891.7 4.3 convert_element_type.12
  896.0 112.6 %all-gather.8.cloned.1.call-done = bf16[2560,3456]{1,0:T(8,128)(2,1)} async-done(((bf16[640,3456]{1,0:T(8,128)(2,1)}), bf16[2560,3456]{1,0:T(8,128)(2,1)}) %all-gather.8.cloned.1.call-update) | async-done | bytes 17694736 | tf_op jit(solution)/shard_map/all_gather | solution.py:40
  1008.6 16.0 %copy.12 = bf16[2560,3456]{1,0:T(8,128)(2,1)} copy(bf16[2560,3456]{1,0:T(8,128)(2,1)} %all-gather.8.cloned.1.call-done) | data formatting | bytes 35389440
Async XLA Ops:
  7.2 174.9 %all-gather.4.cloned.1.call-start = ((), (), s32[]{:S(2)}) async-start(), calls=%async_computation.2 | async-start | bytes 21233664 | tf_op jit(solution)/shard_map/all_gather | solution.py:13
  7.9 359.6 %all-gather.6.cloned.1.call-start = ((), (), s32[]{:S(2)}) async-start(), calls=%async_computation.4 | async-start | bytes 13107200 | tf_op jit(solution)/shard_map/all_gather | solution.py:11
  8.6 533.5 %reduce-scatter.5.cloned.1.call-start = ((), (), s32[]{:S(2)}) async-start(), calls=%async_computation.5 | async-start | bytes 22118400 | tf_op jit(solution)/shard_map/reduce_scatter | solution.py:24
  413.2 478.6 %reduce-scatter.3.cloned.1.call-start = ((), (), s32[]{:S(2)}) async-start(), calls=%async_computation.3 | async-start | bytes 26214400 | tf_op jit(solution)/shard_map/reduce_scatter | solution.py:15
  460.5 548.0 %all-gather.8.cloned.1.call-start = ((), (), s32[]{:S(2)}) async-start(), calls=%async_computation.6 | async-start | bytes 22118400 | tf_op jit(solution)/shard_map/all_gather | solution.py:40
Sparse Core Ops, SparseCore 0:
  9.5 172.4 all-gather.3
  183.6 183.8 all-gather.5
  413.3 128.7 reduce-scatter.4
  544.3 347.3 reduce-scatter.2
  893.7 114.7 all-gather.7
where the time goes:
time: 1030 us
  waiting for transfers between devices  881 us (86%)
  matrix products  92.9 us (9%)
  other arithmetic  27.3 us (3%)
  local copies, waits for them, and re-layouts  16 us (2%)
  between operations  13.8 us (1%)
    reduce_scatter x1, waiting for transfers between devices, per_device(): lax.psum_scatter(lax.dot_general(picked, weight, (((1,), (1,)), ((), ()))...  327 us
    all_gather x1, waiting for transfers between devices, per_device(): whole_acts = lax.all_gather(acts, 'col', axis=0, tiled=True)  185 us
    all_gather x1, waiting for transfers between devices, per_device(): whole_cotangent = lax.all_gather(grad_out, 'row', axis=0, tiled=True)  173 us
    all_gather x1, waiting for transfers between devices, per_device(): lax.all_gather(new_master.astype(jnp.bfloat16), 'depth', axis=0, tiled=True)  113 us
    reduce_scatter x1, waiting for transfers between devices, per_device(): lax.psum_scatter(lax.dot_general(picked, whole_cotangent, (((0,), (0,)),...  81.3 us
    dot_general x1, matrix products, per_device(): lax.dot_general(picked, weight, (((1,), (1,)), ((), ())), preferred_eleme...  47.3 us
    dot_general x1, matrix products, per_device(): lax.dot_general(picked, whole_cotangent, (((0,), (0,)), ((), ())), prefer...  45.6 us
    convert_element_type x1, other arithmetic, per_device(): new_master.astype(jnp.bfloat16)  23 us
  transfers between devices with their start and end apart: 5, of which 5 were waited for; matrix products, arithmetic and copies ran while one was open for 7% of the time, Pallas kernels for 0%

commit v1 on v0

--- a/solution.py
+++ b/solution.py
@@ -8,7 +8,12 @@
 
 
 def per_device(acts, grad_out, weight, master, moment_one, moment_two):
-    whole_acts = lax.all_gather(acts, "col", axis=0, tiled=True)
+    ring = [acts]
+    for hop in range(3):
+        ring.append(lax.ppermute(ring[-1], "col", [(dev, (dev + 1) % 4) for dev in range(4)]))
+    whole_acts = jnp.roll(
+        jnp.concatenate(ring[::-1], axis=0), (lax.axis_index("col") + 1) * ring[0].shape[0], axis=0
+    )
     tokens_total = acts.shape[0] * lax.axis_size("col") * lax.axis_size("depth")
     whole_cotangent = lax.all_gather(grad_out, "row", axis=0, tiled=True)
     picked = whole_cotangent

time: 1030 us -> 875 us (0.85)
  waiting for transfers between devices: 881 us -> 699 us
  local copies, waits for them, and re-layouts: 16 us -> 37.8 us
    all_gather x1 -> x0, waiting for transfers between devices: 185 us -> none  [per_device(): whole_acts = lax.all_gather(acts, 'col', axis=0, tiled=True)]
    ppermute x0 -> x3, waiting for transfers between devices: none -> 178 us  [per_device(): lax.ppermute(ring[-1], 'col', [(dev, (dev + 1) % 4) for dev in range(4)])]
    all_gather x1, waiting for transfers between devices: 173 us -> 0.01 us  [per_device(): whole_cotangent = lax.all_gather(grad_out, 'row', axis=0, tiled=True)]
    unnamed x1 -> x14, local copies, waits for them, and re-layouts: 16 us -> 36.2 us
  transfers between devices with their start and end apart: 5 -> 7, of which waited for: 5 -> 6; matrix products, arithmetic and copies ran while one was open for 7% -> 11% of each run, Pallas kernels for 0% -> 0%
where the time goes in v1:
time: 875 us; the launch traced here: 874 us
  waiting for transfers between devices  699 us (80%)
  matrix products  93.3 us (11%)
  local copies, waits for them, and re-layouts  37.8 us (4%)
  other arithmetic  27.3 us (3%)
  between operations  13.8 us (2%)
    reduce_scatter x1, waiting for transfers between devices, per_device(): lax.psum_scatter(lax.dot_general(picked, weight, (((1,), (1,)), ((), ()))...  327 us
    ppermute x3, waiting for transfers between devices, per_device(): lax.ppermute(ring[-1], 'col', [(dev, (dev + 1) % 4) for dev in range(4)])  178 us
    all_gather x1, waiting for transfers between devices, per_device(): lax.all_gather(new_master.astype(jnp.bfloat16), 'depth', axis=0, tiled=True)  113 us
    reduce_scatter x1, waiting for transfers between devices, per_device(): lax.psum_scatter(lax.dot_general(picked, whole_cotangent, (((0,), (0,)),...  80.6 us
    dot_general x1, matrix products, per_device(): lax.dot_general(picked, weight, (((1,), (1,)), ((), ())), preferred_eleme...  47.7 us
    dot_general x1, matrix products, per_device(): lax.dot_general(picked, whole_cotangent, (((0,), (0,)), ((), ())), prefer...  45.6 us
    unnamed x14, local copies, waits for them, and re-layouts  36.2 us
    convert_element_type x1, other arithmetic, per_device(): new_master.astype(jnp.bfloat16)  23 us
  transfers between devices with their start and end apart: 7, of which 6 were waited for; matrix products, arithmetic and copies ran while one was open for 11% of the time, Pallas kernels for 0%

profile of v1, /device:TPU:0, one launch (start us, length us, event | category | flops | bytes accessed | tf_op | source)
XLA Modules:
  0.0 874.5 jit_solution(2497465985580016966)
XLA Ops:
  7.2 0.7 all-gather.3.cloned.1.call-update
  8.0 3.1 collective-permute-start
  11.1 59.1 %collective-permute-done = bf16[512,2560]{1,0:T(8,128)(2,1)S(1)} collective-permute-done((bf16[512,2560]{1,0:T(8,128)(2,1)}, bf16[512,2560]{1,0:T(8,128)(2,1)S(1)}, u32[]{:S(2)}, u32[]{:S(2)}) %collective-permute-start) | collective-permute-done | bytes 2621472 | tf_op jit(solution)/shard_map/ppermute | solution.py:13
  70.2 1.5 copy-done.1
  71.7 59.9 %collective-permute-done.1 = bf16[512,2560]{1,0:T(8,128)(2,1)} collective-permute-done((bf16[512,2560]{1,0:T(8,128)(2,1)S(1)}, bf16[512,2560]{1,0:T(8,128)(2,1)}, u32[]{:S(2)}, u32[]{:S(2)}) %collective-permute-start.1) | collective-permute-done | bytes 2621472 | tf_op jit(solution)/shard_map/ppermute | solution.py:13
  131.6 59.3 %collective-permute-done.2 = bf16[512,2560]{1,0:T(8,128)(2,1)} collective-permute-done((bf16[512,2560]{1,0:T(8,128)(2,1)}, bf16[512,2560]{1,0:T(8,128)(2,1)}, u32[]{:S(2)}, u32[]{:S(2)}) %collective-permute-start.2) | collective-permute-done | bytes 2621472 | tf_op jit(solution)/shard_map/ppermute | solution.py:13
  190.9 3.4 constant_dynamic-update-slice_fusion.7
  194.3 3.4 constant_dynamic-update-slice_fusion.6
  197.7 1.6 constant_dynamic-update-slice_fusion.5
  199.4 1.7 constant_dynamic-update-slice_fusion.4
  201.1 3.5 constant_dynamic-update-slice_fusion.3
  204.5 3.4 constant_dynamic-update-slice_fusion.2
  207.9 1.7 constant_dynamic-update-slice_fusion.1
  209.6 1.6 constant_dynamic-update-slice_fusion
  211.2 45.6 %convolution_convert_fusion = bf16[2560,3456]{1,0:T(8,128)(2,1)} fusion(bf16[2048,3456]{1,0:T(8,128)(2,1)} %all-gather.3.cloned.1.call-done, bf16[4096,2560]{1,0:T(8,128)(2,1)} %constant_dynamic-update-slice_fusion, s32[]{:T(128)S(6)} %select_n.14), kind=kOutput, calls=%fused_computation | convolution fusion | flops 36247633920 | bytes 42336260 | tf_op jit(solution)/shard_map/dot_general | solution.py:30
  256.8 0.0 reduce-scatter.3.cloned.1.call-start
  256.9 47.7 %fusion.8 = f32[2048,2560]{1,0:T(8,128)} fusion(bf16[2048,3456]{1,0:T(8,128)(2,1)} %all-gather.3.cloned.1.call-done, bf16[2560,3456]{1,0:T(8,128)(2,1)} %param.8), kind=kOutput, calls=%fused_computation.19 | convolution fusion | flops 36238786560 | bytes 52822016 | tf_op jit(solution)/shard_map/dot_general | solution.py:21
  304.6 0.2 all-gather.5.cloned.1.call-start
  304.8 80.6 %reduce-scatter.5.cloned.1.call-done = bf16[640,3456]{1,0:T(8,128)(2,1)} async-done(((bf16[2560,3456]{1,0:T(8,128)(2,1)}), bf16[640,3456]{1,0:T(8,128)(2,1)}) %reduce-scatter.5.cloned.1.call-update) | async-done | bytes 4423696 | tf_op jit(solution)/shard_map/reduce_scatter | solution.py:29
  385.4 23.0 %fusion.5 = (bf16[640,3456]{1,0:T(8,128)(2,1)}, f32[640,3456]{1,0:T(8,128)}, f32[640,3456]{1,0:T(8,128)}, f32[640,3456]{1,0:T(8,128)}) fusion(f32[640,3456]{1,0:T(8,128)} %param.9, bf16[640,3456]{1,0:T(8,128)(2,1)} %reduce-scatter.5.cloned.1.call-done, f32[640,3456]{1,0:T(8,128)} %param.10, f32[640,3456]{1,0:T(8,128)} %param.11), kind=kLoop, calls=%fused_computation.18 | loop fusion | flops 39813120 | bytes 61931520 | tf_op jit(solution)/shard_map/convert_element_type | solution.py:45
  408.4 326.7 %reduce-scatter.3.cloned.1.call-done = f32[512,2560]{1,0:T(8,128)} async-done(((f32[2048,2560]{1,0:T(8,128)}), f32[512,2560]{1,0:T(8,128)}) %reduce-scatter.3.cloned.1.call-update) | async-done | bytes 5242896 | tf_op jit(solution)/shard_map/reduce_scatter | solution.py:20
  735.1 4.3 convert_element_type.12
  739.4 112.5 %all-gather.5.cloned.1.call-done = bf16[2560,3456]{1,0:T(8,128)(2,1)} async-done(((bf16[640,3456]{1,0:T(8,128)(2,1)}), bf16[2560,3456]{1,0:T(8,128)(2,1)}) %all-gather.5.cloned.1.call-update) | async-done | bytes 17694736 | tf_op jit(solution)/shard_map/all_gather | solution.py:45
  851.9 16.0 %copy.19 = bf16[2560,3456]{1,0:T(8,128)(2,1)} copy(bf16[2560,3456]{1,0:T(8,128)(2,1)} %all-gather.5.cloned.1.call-done) | data formatting | bytes 35389440
  (13 shorter events, 0.1 us)
Async XLA Ops:
  7.2 204.0 %all-gather.3.cloned.1.call-start = ((), (), s32[]{:S(2)}) async-start(), calls=%async_computation.2 | async-start | bytes 21233664 | tf_op jit(solution)/shard_map/all_gather | solution.py:18
  7.9 191.5 %copy-start = (bf16[512,2560]{1,0:T(8,128)(2,1)S(1)}, bf16[512,2560]{1,0:T(8,128)(2,1)}, u32[]{:S(2)}) copy-start(bf16[512,2560]{1,0:T(8,128)(2,1)} %param.6) | copy-start | bytes 7864324
  7.9 377.5 %reduce-scatter.5.cloned.1.call-start = ((), (), s32[]{:S(2)}) async-start(), calls=%async_computation.4 | async-start | bytes 22118400 | tf_op jit(solution)/shard_map/reduce_scatter | solution.py:29
  8.0 62.2 %collective-permute-start = (bf16[512,2560]{1,0:T(8,128)(2,1)}, bf16[512,2560]{1,0:T(8,128)(2,1)S(1)}, u32[]{:S(2)}, u32[]{:S(2)}) collective-permute-start(bf16[512,2560]{1,0:T(8,128)(2,1)} %param.6), channel_id=1, source_target_pairs={{0,4},{4,8},{8,12},{12,0},{1,5},{5,9},{9,13},{13,1},{2,6},{6,10},{... | collective-permute-start | bytes 7864328 | tf_op jit(solution)/shard_map/ppermute | solution.py:13
  70.2 1.5 copy-start.1
  71.7 59.9 %collective-permute-start.1 = (bf16[512,2560]{1,0:T(8,128)(2,1)S(1)}, bf16[512,2560]{1,0:T(8,128)(2,1)}, u32[]{:S(2)}, u32[]{:S(2)}) collective-permute-start(bf16[512,2560]{1,0:T(8,128)(2,1)S(1)} %collective-permute-done), channel_id=1, source_target_pairs={{0,4},{4,8},{8,12},{12,0},{1,5},{5,9},{9,13},{13,1},{2,6},{6,10},{... | collective-permute-start | bytes 7864328 | tf_op jit(solution)/shard_map/ppermute | solution.py:13
  131.6 59.3 %collective-permute-start.2 = (bf16[512,2560]{1,0:T(8,128)(2,1)}, bf16[512,2560]{1,0:T(8,128)(2,1)}, u32[]{:S(2)}, u32[]{:S(2)}) collective-permute-start(bf16[512,2560]{1,0:T(8,128)(2,1)} %collective-permute-done.1), channel_id=1, source_target_pairs={{0,4},{4,8},{8,12},{12,0},{1,5},{5,9},{9,13},{13,1},{2,6},{6,10},{... | collective-permute-start | bytes 7864328 | tf_op jit(solution)/shard_map/ppermute | solution.py:13
  131.6 66.1 %copy-start.2 = (bf16[512,2560]{1,0:T(8,128)(2,1)S(1)}, bf16[512,2560]{1,0:T(8,128)(2,1)}, u32[]{:S(2)}) copy-start(bf16[512,2560]{1,0:T(8,128)(2,1)} %copy-done.1) | copy-start | bytes 7864324
  256.8 478.3 %reduce-scatter.3.cloned.1.call-start = ((), (), s32[]{:S(2)}) async-start(), calls=%async_computation.3 | async-start | bytes 26214400 | tf_op jit(solution)/shard_map/reduce_scatter | solution.py:20
  304.6 547.4 %all-gather.5.cloned.1.call-start = ((), (), s32[]{:S(2)}) async-start(), calls=%async_computation.5 | async-start | bytes 22118400 | tf_op jit(solution)/shard_map/all_gather | solution.py:45
Sparse Core Ops, SparseCore 0:
  9.5 172.4 all-gather.2
  257.0 128.3 reduce-scatter.4
  387.7 347.3 reduce-scatter.2
  737.1 114.7 all-gather.4
